TPU v7x, 32 devices: a whole 2x2x4 slice. The times are simulated.
32 devices in a mesh: tm: 8 (over z, y), space: 4 (over x, core).
Axes of the slice: x: 2, y: 2, z: 4, core: 2. Of those that a mesh axis runs over, the one named last changes fastest.
Arguments:
- starts: float32 [8, 5, 16, 64, 128], P('tm', None, 'space'), may hold values from -4 to 4
- source: float32 [5, 16, 64, 128], P(None, 'space'), may hold values from -4 to 4
Outputs:
- ends: float32 [8, 5, 16, 64, 128], P('tm', None, 'space')
- slice_norms: float32 [8], P('tm')
- total_norm: float32 [1], replicated
All inputs are finite; a program needn't handle non-finite values.
Results may differ from a plain program's by a relative error of at most 0.0003.
Values sent between devices are 32-bit elements; how exact they have to be, the bound alone decides.
A program may use at most 64 MiB of HBM per device.

v0:
```python
import math

import jax
import jax.numpy as jnp
from jax import lax
from jax.sharding import PartitionSpec as P

viscosity = 0.08
diffusivity = 0.05
compress_rate = 0.25
time_step = 0.5
diffusion_number = 0.08
advect_xaxis = 0.2
advect_yaxis = 0.15
advect_zaxis = 0.1
epsilon = 1e-06
highest = lax.Precision.HIGHEST


def with_halo(cells, sides, width):
    for axis, dim in sides:
        count = lax.axis_size(axis)
        head = lax.slice_in_dim(cells, 0, width, axis=dim)
        tail = lax.slice_in_dim(cells, cells.shape[dim] - width, cells.shape[dim], axis=dim)
        cells = jnp.concatenate(
            [
                lax.ppermute(tail, axis, [(i, (i + 1) % count) for i in range(count)]),
                cells,
                lax.ppermute(head, axis, [((i + 1) % count, i) for i in range(count)]),
            ],
            axis=dim,
        )
    return cells


def across(values, axis):
    return 0.5 * (jnp.roll(values, -1, axis) - jnp.roll(values, 1, axis))


def vertical(values):
    return 0.5 * (values[2:] - values[:-2])


def laplace(values):
    interior = values[1:-1]
    summed = values[2:] + values[:-2] - 6.0 * interior
    for axis in (1, 2):
        summed = summed + jnp.roll(interior, -1, axis) + jnp.roll(interior, 1, axis)
    return summed


def tendency(padded, source):
    speed_xaxis = advect_xaxis + padded[0]
    speed_yaxis = advect_yaxis + padded[1]
    speed_zaxis = advect_zaxis + padded[2]

    def transport(quantity):
        return (
            across((speed_xaxis * quantity)[1:-1], 2)
            + across((speed_yaxis * quantity)[1:-1], 1)
            + vertical(speed_zaxis * quantity)
        )

    pressure = padded[3]
    xmomentum = -transport(padded[0]) - across(pressure[1:-1], 2) + viscosity * laplace(padded[0])
    ymomentum = -transport(padded[1]) - across(pressure[1:-1], 1) + viscosity * laplace(padded[1])
    zmomentum = -transport(padded[2]) - vertical(pressure) + viscosity * laplace(padded[2])
    pressure_rate = -compress_rate * (
        across(padded[0][1:-1], 2) + across(padded[1][1:-1], 1) + vertical(padded[2])
    )
    scalar_rate = -transport(padded[4]) + diffusivity * laplace(padded[4])
    return jnp.stack([xmomentum, ymomentum, zmomentum, pressure_rate, scalar_rate]) + source


def slab_rates(current, source):
    padded = with_halo(current, (("space", 1),), 1)
    return tendency(padded, source)


def kept_modes(keep):
    mode_ids = jnp.arange(2 * keep, dtype=jnp.int32)
    return jnp.where(mode_ids < keep, mode_ids, mode_ids - 2 * keep)


def wave_table(cell_ids, mode_ids, length):
    products = cell_ids[:, None] * mode_ids[None, :] % length
    angles = 2.0 * math.pi / length * products.astype(jnp.float32)
    return (jnp.cos(angles), jnp.sin(angles))


def shards(starts, source):
    state_now = starts[0]
    fields, slab_depth, grid_rows, grid_cols = state_now.shape
    width_space = lax.axis_size("space")
    width_time = lax.axis_size("tm")
    grid_depth = slab_depth * width_space
    keep_y = grid_rows // 8
    keep_x = grid_cols // 16
    mode_count = 4 * keep_y * keep_x
    current = state_now
    section_one = slab_rates(current, source)
    section_two = slab_rates(current + 0.5 * time_step * section_one, source)
    section_three = slab_rates(current + 0.5 * time_step * section_two, source)
    section_four = slab_rates(current + time_step * section_three, source)
    current = current + time_step / 6.0 * (
        section_one + 2.0 * section_two + 2.0 * section_three + section_four
    )
    xmodes = kept_modes(keep_x)
    ymodes = kept_modes(keep_y)
    xcosines, xsines = wave_table(jnp.arange(grid_cols, dtype=jnp.int32), xmodes, grid_cols)
    ycosines, ysines = wave_table(jnp.arange(grid_rows, dtype=jnp.int32), ymodes, grid_rows)
    stacked = jnp.stack([current, state_now]).reshape(2 * fields, slab_depth, grid_rows, grid_cols)
    real_x = jnp.einsum("bzyx,xk->bzyk", stacked, xcosines, precision=highest)
    imag_x = -jnp.einsum("bzyx,xk->bzyk", stacked, xsines, precision=highest)
    real_y = jnp.einsum("bzyk,yj->bzjk", real_x, ycosines, precision=highest) + jnp.einsum(
        "bzyk,yj->bzjk", imag_x, ysines, precision=highest
    )
    imag_y = jnp.einsum("bzyk,yj->bzjk", imag_x, ycosines, precision=highest) - jnp.einsum(
        "bzyk,yj->bzjk", real_x, ysines, precision=highest
    )
    real_y = real_y.reshape(2 * fields, slab_depth, mode_count)
    imag_y = imag_y.reshape(2 * fields, slab_depth, mode_count)
    space_pos = lax.axis_index("space")
    zcells = space_pos * slab_depth + jnp.arange(slab_depth, dtype=jnp.int32)
    zwaves = jnp.arange(lax.axis_size("space") * slab_depth, dtype=jnp.int32)
    zcosines, zsines = wave_table(zwaves, zcells, grid_depth)
    term_real = jnp.einsum("qz,bzm->qbm", zcosines, real_y, precision=highest) + jnp.einsum(
        "qz,bzm->qbm", zsines, imag_y, precision=highest
    )
    term_imag = jnp.einsum("qz,bzm->qbm", zcosines, imag_y, precision=highest) - jnp.einsum(
        "qz,bzm->qbm", zsines, real_y, precision=highest
    )
    spectrum = lax.psum_scatter(
        jnp.stack([term_real, term_imag], axis=1), "space", scatter_dimension=0, tiled=True
    )
    zangles = 2.0 * math.pi / grid_depth * zcells.astype(jnp.float32)
    yangles = 2.0 * math.pi / grid_rows * ymodes.astype(jnp.float32)
    xangles = 2.0 * math.pi / grid_cols * xmodes.astype(jnp.float32)
    keeper = (
        ((ymodes != -keep_y)[:, None] & (xmodes != -keep_x)[None, :])
        .astype(jnp.float32)
        .reshape(mode_count)
    )
    plane_cos = (
        (2.0 * jnp.cos(yangles) - 2.0)[:, None] + (2.0 * jnp.cos(xangles) - 2.0)[None, :]
    ).reshape(mode_count)
    plane_sin = (
        advect_yaxis * jnp.sin(yangles)[:, None] + advect_xaxis * jnp.sin(xangles)[None, :]
    ).reshape(mode_count)
    sym_real = (
        1.0 + diffusion_number * ((2.0 * jnp.cos(zangles) - 2.0)[:, None] + plane_cos[None, :])
    ) * keeper[None, :]
    sym_imag = -(advect_zaxis * jnp.sin(zangles)[:, None] + plane_sin[None, :]) * keeper[None, :]
    sym_real = sym_real[:, None, :]
    sym_imag = sym_imag[:, None, :]
    log_size = jnp.where(
        keeper[None, None, :] > 0.0,
        0.5 * jnp.log(sym_real * sym_real + sym_imag * sym_imag + (1.0 - keeper[None, None, :])),
        -60.0,
    )
    turning = jnp.arctan2(sym_imag, sym_real)
    fine_real = spectrum[:, 0, :fields]
    fine_imag = spectrum[:, 1, :fields]
    start_real = spectrum[:, 0, fields:]
    start_imag = spectrum[:, 1, fields:]
    position = lax.axis_index("tm")
    later_flag = (position > 0).astype(jnp.float32)
    coarse_real = sym_real * start_real - sym_imag * start_imag
    coarse_imag = sym_real * start_imag + sym_imag * start_real
    jumps = jnp.stack([fine_real - later_flag * coarse_real, fine_imag - later_flag * coarse_imag])
    portion = lax.all_gather(jumps[None], "tm", axis=0, tiled=True)
    source_rows = jnp.arange(portion.shape[0], dtype=jnp.int32)
    gaps = position - 1 - source_rows
    live = (gaps >= 0).astype(jnp.float32)[:, None, None, None]
    exponent = jnp.maximum(gaps, 0).astype(jnp.float32)[:, None, None, None]
    damping = live * jnp.exp(exponent * log_size[None])
    cosine = damping * jnp.cos(exponent * turning[None])
    sine_part = damping * jnp.sin(exponent * turning[None])
    added_real = jnp.sum(cosine * portion[:, 0] - sine_part * portion[:, 1], axis=0)
    added_imag = jnp.sum(cosine * portion[:, 1] + sine_part * portion[:, 0], axis=0)
    prior_sum = jnp.stack([added_real, added_imag])
    diff_real = prior_sum[0] - later_flag * start_real
    diff_imag = prior_sum[1] - later_flag * start_imag
    spectral_fix = jnp.stack(
        [sym_real * diff_real - sym_imag * diff_imag, sym_real * diff_imag + sym_imag * diff_real],
        axis=1,
    )
    portion = lax.all_gather(spectral_fix, "space", axis=0, tiled=True)
    zwaves = jnp.arange(portion.shape[0], dtype=jnp.int32)
    zcosines, zsines = wave_table(zcells, zwaves, grid_depth)
    back_real = jnp.einsum("zq,qfm->zfm", zcosines, portion[:, 0], precision=highest) - jnp.einsum(
        "zq,qfm->zfm", zsines, portion[:, 1], precision=highest
    )
    back_imag = jnp.einsum("zq,qfm->zfm", zcosines, portion[:, 1], precision=highest) + jnp.einsum(
        "zq,qfm->zfm", zsines, portion[:, 0], precision=highest
    )
    local_depth = jnp.stack([back_real, back_imag], axis=1)
    planes = local_depth.reshape(slab_depth, 2, fields, 2 * keep_y, 2 * keep_x)
    plane_real = jnp.einsum(
        "zfjk,yj->zfyk", planes[:, 0], ycosines, precision=highest
    ) - jnp.einsum("zfjk,yj->zfyk", planes[:, 1], ysines, precision=highest)
    plane_imag = jnp.einsum(
        "zfjk,yj->zfyk", planes[:, 1], ycosines, precision=highest
    ) + jnp.einsum("zfjk,yj->zfyk", planes[:, 0], ysines, precision=highest)
    correction = (
        jnp.einsum("zfyk,xk->fzyx", plane_real, xcosines, precision=highest)
        - jnp.einsum("zfyk,xk->fzyx", plane_imag, xsines, precision=highest)
    ) / (grid_depth * grid_rows * grid_cols)
    end_states = current + correction
    local_sum = jnp.sum(correction * correction)
    cell_total = fields * grid_depth * grid_rows * grid_cols
    slice_sum = lax.psum(local_sum, "space")
    every_sum = lax.psum(slice_sum, "tm")
    slice_value = jnp.sqrt(slice_sum / cell_total + epsilon).reshape(1)
    total_value = jnp.sqrt(every_sum / (cell_total * width_time) + epsilon).reshape(1)
    return (end_states[None], slice_value, total_value)


def solution(mesh):
    in_specs = (P("tm", None, "space", None, None), P(None, "space", None, None))
    out_specs = (P("tm", None, "space", None, None), P("tm"), P())
    return jax.shard_map(shards, mesh=mesh, in_specs=in_specs, out_specs=out_specs, check_vma=False)
```

profile of v0, /device:TPU:0, one launch (start us, length us, event | category | flops | bytes accessed | tf_op | source)
XLA Modules:
  0.0 202.2 jit_solution(17779550570251596355)
XLA Ops:
  7.2 1.8 fusion.450
  9.5 1.9 collective-permute-start.1
  11.4 1.2 slice_bitcast_fusion.17
  12.6 0.8 slice_bitcast_fusion.51
  13.4 0.8 slice_bitcast_fusion.50
  14.4 0.8 slice_bitcast_fusion.48
  15.2 0.8 fusion.568
  16.0 0.9 fusion.569
  16.9 0.9 fusion.571
  17.8 0.6 sine_multiply_fusion.2
  19.0 0.6 sine_multiply_fusion
  19.8 0.6 broadcast_subtract_fusion
  20.9 0.7 broadcast_add_fusion.1
  21.7 0.8 broadcast_add_fusion
  22.5 0.7 add.1066
  23.2 0.8 multiply_select_fusion
  24.0 1.2 dynamic-slice
  30.3 0.6 copy-done.13
  31.6 0.8 copy-done.1
  33.7 0.7 collective-permute-start.2
  34.4 1.1 collective-permute-start.3
  35.5 3.0 %collective-permute-done.2 = f32[5,1,64,128]{3,2,1,0:T(8,128)S(1)} collective-permute-done((f32[5,1,64,128]{3,2,1,0:T(8,128)S(1)}, f32[5,1,64,128]{3,2,1,0:T(8,128)S(1)}, u32[]{:S(2)}, u32[]{:S(2)}) %collective-permute-start.2) | collective-permute-done | bytes 163872 | tf_op jit(solution)/shard_map/ppermute | solution.py:27
  38.5 1.6 collective-permute-done.3
  44.1 0.9 collective-permute-start.4
  45.0 1.4 collective-permute-start.5
  46.4 2.9 %collective-permute-done.4 = f32[5,1,64,128]{3,2,1,0:T(8,128)S(1)} collective-permute-done((f32[5,1,64,128]{3,2,1,0:T(8,128)S(1)}, f32[5,1,64,128]{3,2,1,0:T(8,128)S(1)}, u32[]{:S(2)}, u32[]{:S(2)}) %collective-permute-start.4) | collective-permute-done | bytes 163872 | tf_op jit(solution)/shard_map/ppermute | solution.py:27
  49.3 1.3 collective-permute-done.5
  55.2 0.9 collective-permute-start.6
  56.1 1.3 collective-permute-start.7
  57.4 2.8 %collective-permute-done.6 = f32[5,1,64,128]{3,2,1,0:T(8,128)S(1)} collective-permute-done((f32[5,1,64,128]{3,2,1,0:T(8,128)S(1)}, f32[5,1,64,128]{3,2,1,0:T(8,128)S(1)}, u32[]{:S(2)}, u32[]{:S(2)}) %collective-permute-start.6) | collective-permute-done | bytes 163872 | tf_op jit(solution)/shard_map/ppermute | solution.py:27
  60.2 1.2 collective-permute-done.7
  64.5 3.2 %fusion.304 = f32[10,4,64,16]{2,3,1,0:T(8,128)S(1)} fusion(f32[10,4,64,128]{3,2,1,0:T(8,128)S(1)} %bitcast.754, s32[16]{0:T(128)S(1)} %compare_select_fusion), kind=kOutput, calls=%fused_computation.540 | convolution fusion | flops 62943232 | bytes 1474624 | tf_op jit(solution)/shard_map/bzyx,xk->bzyk/dot_general | solution.py:113
  67.7 3.2 %convolution_negate_fusion = f32[10,4,64,16]{2,3,1,0:T(8,128)S(1)} fusion(f32[10,4,64,128]{3,2,1,0:T(8,128)S(1)} %bitcast.755, s32[16]{0:T(128)S(1)} %compare_select_fusion), kind=kOutput, calls=%fused_computation.8 | convolution fusion | flops 62984192 | bytes 1474624 | tf_op jit(solution)/shard_map/bzyx,xk->bzyk/dot_general | solution.py:114
  70.9 2.5 %fusion.310 = f32[16,10,4,16]{3,0,2,1:T(8,128)S(1)} fusion(f32[10,4,64,16]{2,3,1,0:T(8,128)S(1)} %fusion.304, s32[16]{0:T(128)S(1)} %compare_select_fusion), kind=kOutput, calls=%fused_computation.546 | convolution fusion | flops 7878656 | bytes 204864 | tf_op jit(solution)/shard_map/bzyk,yj->bzjk/dot_general | solution.py:115
  73.4 2.5 %fusion.308 = f32[16,10,4,16]{3,0,2,1:T(8,128)S(1)} fusion(f32[10,4,64,16]{2,3,1,0:T(8,128)S(1)} %convolution_negate_fusion, s32[16]{0:T(128)S(1)} %compare_select_fusion), kind=kOutput, calls=%fused_computation.544 | convolution fusion | flops 7878656 | bytes 204864 | tf_op jit(solution)/shard_map/bzyk,yj->bzjk/dot_general | solution.py:118
  75.9 2.5 %fusion.3 = f32[10,4,16,16]{3,2,1,0:T(8,128)S(1)} fusion(f32[16,10,4,16]{3,0,2,1:T(8,128)S(1)} %fusion.310, f32[10,4,64,16]{2,3,1,0:T(8,128)S(1)} %convolution_negate_fusion, s32[16]{0:T(128)S(1)} %compare_select_fusion), kind=kOutput, calls=%fused_computation.7 | convolution fusion | flops 7888896 | bytes 245824 | tf_op jit(solution)/shard_map/bzyk,yj->bzjk/dot_general | solution.py:115
  78.6 2.5 %fusion.2 = f32[10,4,16,16]{3,2,1,0:T(8,128)S(1)} fusion(f32[16,10,4,16]{3,0,2,1:T(8,128)S(1)} %fusion.308, f32[10,4,64,16]{2,3,1,0:T(8,128)S(1)} %fusion.304, s32[16]{0:T(128)S(1)} %compare_select_fusion), kind=kOutput, calls=%fused_computation.5 | convolution fusion | flops 7888896 | bytes 245824 | tf_op jit(solution)/shard_map/bzyk,yj->bzjk/dot_general | solution.py:118
  83.3 0.7 pad_maximum_fusion.1
  84.4 32.7 %all-reduce.3.cloned.1.call-done = f32[16,2,10,256]{3,0,2,1:T(8,128)} async-done(((f32[16,2,10,256]{3,0,2,1:T(8,128)}), f32[16,2,10,256]{3,0,2,1:T(8,128)}) %all-reduce.3.cloned.1.call-update) | async-done | bytes 327696
  117.1 0.9 fusion.285
  118.0 31.1 %all-gather = f32[16,4,5,256]{3,1,2,0:T(4,128)S(1)} all-gather(f32[2,4,5,256]{3,1,2,0:T(4,128)S(1)} %pad_maximum_fusion.26), channel_id=2, replica_groups=mesh['tm'=8,'space'=4] {'tm'}, dimensions={0}, use_global_device_ids=true | all-gather | bytes 368640 | tf_op jit(solution)/shard_map/all_gather | solution.py:171
  149.2 0.8 multiply_subtract_fusion
  150.1 5.7 %all_gather.7 = f32[16,2,5,256]{3,1,2,0:T(2,128)S(1)} all-gather(f32[4,2,5,256]{3,1,2,0:T(2,128)S(1)} %copy.243), channel_id=1, replica_groups=mesh['tm'=8,'space'=4] {'space'}, dimensions={0}, use_global_device_ids=true | all-gather | bytes 204800 | tf_op jit(solution)/shard_map/all_gather | solution.py:188
  159.3 1.2 fusion.302
  160.5 1.8 multiply_reduce_fusion
  162.4 6.6 %psum.14 = f32[]{:T(128)} all-reduce(f32[]{:T(128)} %get-tuple-element.60), channel_id=1, replica_groups=mesh['tm'=8,'space'=4] {'space'}, use_global_device_ids=true, to_apply=%region_4.5 | all-reduce | flops 1 | bytes 8 | tf_op jit(solution)/shard_map/psum | solution.py:212
  169.0 0.9 copy.250
  169.9 21.8 %psum.15 = f32[]{:T(128)} all-reduce(f32[]{:T(128)} %psum.14), channel_id=1, replica_groups=mesh['tm'=8,'space'=4] {'tm'}, use_global_device_ids=true, to_apply=%region_5.6 | all-reduce | flops 1 | bytes 8 | tf_op jit(solution)/shard_map/psum | solution.py:213
  (245 shorter events, 25.1 us)
Async XLA Ops:
  7.2 110.0 %all-reduce.3.cloned.1.call-start = ((), (), s32[]{:S(2)}) async-start(), calls=%async_computation | async-start | bytes 655360
  9.0 17.5 %collective-permute-start = (f32[5,1,64,128]{3,2,1,0:T(8,128)}, f32[5,1,64,128]{3,2,1,0:T(8,128)S(1)}, u32[]{:S(2)}, u32[]{:S(2)}) collective-permute-start(f32[5,1,64,128]{3,2,1,0:T(8,128)} %get-tuple-element.91), channel_id=1, source_target_pairs={{0,1},{1,2},{2,3},{3,0},{4,5},{5,6},{6,7},{7,4},{8,9},{9,10},{10,1... | collective-permute-start | bytes 491528 | tf_op jit(solution)/shard_map/ppermute | solution.py:27
  9.5 17.0 %collective-permute-start.1 = (f32[5,1,64,128]{3,2,1,0:T(8,128)}, f32[5,1,64,128]{3,2,1,0:T(8,128)S(1)}, u32[]{:S(2)}, u32[]{:S(2)}) collective-permute-start(f32[5,1,64,128]{3,2,1,0:T(8,128)} %get-tuple-element.90), channel_id=1, source_target_pairs={{1,0},{2,1},{3,2},{0,3},{5,4},{6,5},{7,6},{4,7},{9,8},{10,9},{11,1... | collective-permute-start | bytes 491528 | tf_op jit(solution)/shard_map/ppermute | solution.py:29
  16.0 10.4 %copy-start = (f32[1,5,4,64,128]{4,3,2,1,0:T(8,128)S(1)}, f32[1,5,4,64,128]{4,3,2,1,0:T(8,128)}, u32[]{:S(2)}) copy-start(f32[1,5,4,64,128]{4,3,2,1,0:T(8,128)} %param.2) | copy-start | bytes 1966084
  27.6 0.9 copy-start.7
  27.6 1.0 copy-start.8
  27.6 1.0 copy-start.9
  27.7 1.1 copy-start.10
  27.7 1.1 copy-start.11
  27.7 1.2 copy-start.12
  28.8 0.9 copy-start.2
  28.8 1.0 copy-start.3
  28.8 1.0 copy-start.4
  28.8 1.1 copy-start.5
  28.9 1.2 copy-start.6
  30.0 0.9 copy-start.13
  30.0 1.0 copy-start.14
  30.0 1.0 copy-start.15
  30.0 1.1 copy-start.16
  30.0 1.2 copy-start.17
  30.0 1.2 copy-start.18
  31.4 1.1 copy-start.1
  33.7 4.8 %collective-permute-start.2 = (f32[5,1,64,128]{3,2,1,0:T(8,128)S(1)}, f32[5,1,64,128]{3,2,1,0:T(8,128)S(1)}, u32[]{:S(2)}, u32[]{:S(2)}) collective-permute-start(f32[5,1,64,128]{3,2,1,0:T(8,128)S(1)} %get-tuple-element.84), channel_id=1, source_target_pairs={{0,1},{1,2},{2,3},{3,0},{4,5},{5,6},{6,7},{7,4},{8,9},{9,10},{10,1... | collective-permute-start | bytes 491528 | tf_op jit(solution)/shard_map/ppermute | solution.py:27
  34.4 5.7 %collective-permute-start.3 = (f32[5,1,64,128]{3,2,1,0:T(8,128)S(1)}, f32[5,1,64,128]{3,2,1,0:T(8,128)S(1)}, u32[]{:S(2)}, u32[]{:S(2)}) collective-permute-start(f32[5,1,64,128]{3,2,1,0:T(8,128)S(1)} %get-tuple-element.83), channel_id=1, source_target_pairs={{1,0},{2,1},{3,2},{0,3},{5,4},{6,5},{7,6},{4,7},{9,8},{10,9},{11,1... | collective-permute-start | bytes 491528 | tf_op jit(solution)/shard_map/ppermute | solution.py:29
  44.1 5.2 %collective-permute-start.4 = (f32[5,1,64,128]{3,2,1,0:T(8,128)S(1)}, f32[5,1,64,128]{3,2,1,0:T(8,128)S(1)}, u32[]{:S(2)}, u32[]{:S(2)}) collective-permute-start(f32[5,1,64,128]{3,2,1,0:T(8,128)S(1)} %get-tuple-element.76), channel_id=1, source_target_pairs={{0,1},{1,2},{2,3},{3,0},{4,5},{5,6},{6,7},{7,4},{8,9},{9,10},{10,1... | collective-permute-start | bytes 491528 | tf_op jit(solution)/shard_map/ppermute | solution.py:27
  45.0 5.6 %collective-permute-start.5 = (f32[5,1,64,128]{3,2,1,0:T(8,128)S(1)}, f32[5,1,64,128]{3,2,1,0:T(8,128)S(1)}, u32[]{:S(2)}, u32[]{:S(2)}) collective-permute-start(f32[5,1,64,128]{3,2,1,0:T(8,128)S(1)} %get-tuple-element.75), channel_id=1, source_target_pairs={{1,0},{2,1},{3,2},{0,3},{5,4},{6,5},{7,6},{4,7},{9,8},{10,9},{11,1... | collective-permute-start | bytes 491528 | tf_op jit(solution)/shard_map/ppermute | solution.py:29
  55.2 5.0 %collective-permute-start.6 = (f32[5,1,64,128]{3,2,1,0:T(8,128)S(1)}, f32[5,1,64,128]{3,2,1,0:T(8,128)S(1)}, u32[]{:S(2)}, u32[]{:S(2)}) collective-permute-start(f32[5,1,64,128]{3,2,1,0:T(8,128)S(1)} %get-tuple-element.68), channel_id=1, source_target_pairs={{0,1},{1,2},{2,3},{3,0},{4,5},{5,6},{6,7},{7,4},{8,9},{9,10},{10,1... | collective-permute-start | bytes 491528 | tf_op jit(solution)/shard_map/ppermute | solution.py:27
  56.1 5.3 %collective-permute-start.7 = (f32[5,1,64,128]{3,2,1,0:T(8,128)S(1)}, f32[5,1,64,128]{3,2,1,0:T(8,128)S(1)}, u32[]{:S(2)}, u32[]{:S(2)}) collective-permute-start(f32[5,1,64,128]{3,2,1,0:T(8,128)S(1)} %get-tuple-element.67), channel_id=1, source_target_pairs={{1,0},{2,1},{3,2},{0,3},{5,4},{6,5},{7,6},{4,7},{9,8},{10,9},{11,1... | collective-permute-start | bytes 491528 | tf_op jit(solution)/shard_map/ppermute | solution.py:29
  81.1 3.0 %copy-start.19 = (f32[8]{0:T(128)S(1)}, f32[8]{0:T(128)}, u32[]{:S(2)}) copy-start(f32[8]{0:T(128)} %maximum_convert_fusion) | copy-start | bytes 100
Sparse Core Ops, SparseCore 0:
  84.2 32.9 all-reduce.2
where the time goes:
time: 203 us; the launch traced here: 202 us
  blocking collectives  65.3 us (32%)
  waiting for transfers between devices  45.6 us (22%)
  matrix products  24.5 us (12%)
  local copies, waits for them, and re-layouts  22.2 us (11%)
  between operations  19.9 us (10%)
  other arithmetic  16 us (8%)
  starting transfers between devices  8.72 us (4%)
    unnamed x2, waiting for transfers between devices  32.7 us
    all_gather x1, blocking collectives, shards(): portion = lax.all_gather(jumps[None], 'tm', axis=0, tiled=True)  31.1 us
    psum x1, blocking collectives, shards(): every_sum = lax.psum(slice_sum, 'tm')  21.8 us
    ppermute x4, waiting for transfers between devices, with_halo(): lax.ppermute(tail, axis, [(i, (i + 1) % count) for i in range(count)])  8.68 us
    psum x1, blocking collectives, shards(): slice_sum = lax.psum(local_sum, 'space')  6.61 us
    all_gather x1, blocking collectives, shards(): portion = lax.all_gather(spectral_fix, 'space', axis=0, tiled=True)  5.73 us
    ppermute x4, starting transfers between devices, with_halo(): lax.ppermute(head, axis, [((i + 1) % count, i) for i in range(count)])  5.7 us
    unnamed x42, local copies, waits for them, and re-layouts  5.61 us
  transfers between devices with their start and end apart: 9, of which 7 were waited for; matrix products, arithmetic and copies ran while one was open for 7% of the time, Pallas kernels for 0%

commit v1 on v0

v1 whole, which is shorter than its diff:
```python
import functools
import math

import jax
import jax.numpy as jnp
import numpy as np
from jax import lax
from jax.experimental import pallas as pl
from jax.experimental.pallas import tpu as pltpu
from jax.sharding import PartitionSpec as P

viscosity = 0.08
diffusivity = 0.05
compress_rate = 0.25
time_step = 0.5
diffusion_number = 0.08
advect_xaxis = 0.2
advect_yaxis = 0.15
advect_zaxis = 0.1
epsilon = 1e-06
MESH = pl.DeviceIdType.MESH
PAD = 8
CHUNK = 16
LANES = 128


def tables(depth, rows, cols, spaces):
    keep_y, keep_x = rows // 8, cols // 16
    slot = 2 * keep_x
    per = LANES // (slot * depth)
    full = depth * spaces
    k = np.arange(keep_x)
    x = np.arange(cols)
    ax = 2 * math.pi / cols * ((x[:, None] * k[None, :]) % cols)
    weight = np.where(k == 0, 1.0, 2.0) / (full * rows * cols)
    xf = np.zeros((2 * cols, LANES))
    xi = np.zeros((LANES, 2 * cols))
    for i in range(2):
        at = i * slot
        xf[i * cols : (i + 1) * cols, at : at + keep_x] = np.cos(ax)
        xf[i * cols : (i + 1) * cols, at + keep_x : at + slot] = -np.sin(ax)
        xi[at : at + keep_x, i * cols : (i + 1) * cols] = (np.cos(ax) * weight).T
        xi[at + keep_x : at + slot, i * cols : (i + 1) * cols] = (-np.sin(ax) * weight).T
    ky = np.arange(2 * keep_y)
    ky = np.where(ky < keep_y, ky, ky - 2 * keep_y)
    y = np.arange(rows)
    ay = 2 * math.pi / rows * ((ky[:, None] * y[None, :]) % rows)
    yf = np.concatenate([np.cos(ay), np.sin(ay)], axis=1)
    yi = np.concatenate([np.cos(ay).T, -np.sin(ay).T], axis=1)
    kz = np.arange(full)
    width = full * keep_x
    half = depth * slot
    zf = np.zeros((LANES, per * 2 * width))
    for fp in range(per):
        for z in range(depth):
            a = 2 * math.pi / full * ((kz * z) % full)
            for kk in range(keep_x):
                row = fp * half + z * slot + kk
                re = fp * 2 * width + kz * keep_x + kk
                im = re + width
                zf[row, re] = np.cos(a)
                zf[row, im] = -np.sin(a)
                zf[row + keep_x, re] = np.sin(a)
                zf[row + keep_x, im] = np.cos(a)
    zi = np.zeros((2 * width, full * slot))
    for z in range(full):
        a = 2 * math.pi / full * ((kz * z) % full)
        for kk in range(keep_x):
            re = kz * keep_x + kk
            im = re + width
            col = z * slot + kk
            zi[re, col] = np.cos(a)
            zi[im, col] = -np.sin(a)
            zi[re, col + keep_x] = np.sin(a)
            zi[im, col + keep_x] = np.cos(a)
    tz = 2 * math.pi / full * kz
    ty = 2 * math.pi / rows * ky
    tx = 2 * math.pi / cols * k
    live = (ky != -keep_y).astype(np.float64)[:, None, None]
    real = 1.0 + diffusion_number * (
        (2 * np.cos(ty) - 2)[:, None, None]
        + (2 * np.cos(tz) - 2)[None, :, None]
        + (2 * np.cos(tx) - 2)[None, None, :]
    )
    imag = -(
        advect_yaxis * np.sin(ty)[:, None, None]
        + advect_zaxis * np.sin(tz)[None, :, None]
        + advect_xaxis * np.sin(tx)[None, None, :]
    )
    symbol = np.stack([real * live, imag * live]).reshape(2, 2 * keep_y, width)
    return [xf, yf, zf, zi, yi, xi], symbol.astype(np.float32)


def halves(table):
    high = table.astype(jnp.bfloat16)
    low = (table - high.astype(np.float64)).astype(jnp.bfloat16)
    return np.stack([high, low])


def split(values):
    high = values.astype(jnp.bfloat16)
    return high, (values - high.astype(jnp.float32)).astype(jnp.bfloat16)


def dot(a, b):
    return jnp.dot(a, b, preferred_element_type=jnp.float32)


def times(values, table):
    high, low = split(values)
    return dot(high, table[0]) + dot(low, table[0]) + dot(high, table[1])


def under(table, values):
    high, low = split(values)
    return dot(table[0], high) + dot(table[0], low) + dot(table[1], high)


def kernel(
    sizes, starts, source, xf_h, yf_h, zf_h, zi_h, yi_h, xi_h, sym_h,
    ends, slice_out, total_out,
    y1, y2, y3, y4, src, fine, halo, xf, yf, zf, zi, yi, xi, sym,
    own, jumps, ahead, mode_send, mode_recv, square_send, squares,
    load_sem, table_sem, halo_send, halo_recv, ahead_sems, jump_send, jump_recv,
    mode_ssem, mode_rsem, sq_send, sq_recv, out_sem,
):
    times_n, spaces, fields, depth, rows, cols = sizes
    keep_y, keep_x = rows // 8, cols // 16
    slot = 2 * keep_x
    ky = 2 * keep_y
    layers = fields * depth
    slots = LANES // slot
    groups = -(-layers // slots)
    per = LANES // (slot * depth)
    chunks = rows // CHUNK
    devices = times_n * spaces
    n = lax.axis_index("tm")
    s = lax.axis_index("space")
    me = n * spaces + s
    up = lax.rem(s + 1, spaces)
    down = lax.rem(s + spaces - 1, spaces)

    barrier = pltpu.get_barrier_semaphore()

    def greet(i, c):
        @pl.when(i != me)
        def _():
            pl.semaphore_signal(
                barrier, inc=1, device_id=(i // spaces, lax.rem(i, spaces)), device_id_type=MESH
            )

        return c

    lax.fori_loop(0, devices, greet, 0)
    loads = [
        pltpu.make_async_copy(starts.at[0], y1.at[:, :, pl.ds(PAD, rows)], load_sem.at[0]),
        pltpu.make_async_copy(
            starts.at[0, :, :, pl.ds(rows - PAD, PAD)], y1.at[:, :, pl.ds(0, PAD)], load_sem.at[1]
        ),
        pltpu.make_async_copy(
            starts.at[0, :, :, pl.ds(0, PAD)], y1.at[:, :, pl.ds(PAD + rows, PAD)], load_sem.at[2]
        ),
        pltpu.make_async_copy(source, src, load_sem.at[3]),
    ]
    for copy in loads:
        copy.start()
    fills = [
        pltpu.make_async_copy(a, b, table_sem.at[i])
        for i, (a, b) in enumerate(
            [(xf_h, xf), (yf_h, yf), (zf_h, zf), (zi_h, zi), (yi_h, yi), (xi_h, xi), (sym_h, sym)]
        )
    ]
    for copy in fills:
        copy.start()
    for copy in loads:
        copy.wait()
    pl.semaphore_wait(barrier, devices - 1)

    states = [y1, y2, y3, y4]

    def halo_copy(stage, side, chunk):
        r0 = pl.multiple_of(chunk * CHUNK, CHUNK)
        state = states[stage]
        layer = depth - 1 if side == 0 else 0
        return pltpu.make_async_remote_copy(
            src_ref=state.at[:, layer, pl.ds(pl.multiple_of(PAD + r0, 8), CHUNK)],
            dst_ref=halo.at[stage, side, :, pl.ds(r0, CHUNK)],
            send_sem=halo_send.at[stage, side, chunk],
            recv_sem=halo_recv.at[stage, side, chunk],
            device_id=(n, up if side == 0 else down),
            device_id_type=MESH,
        )

    def send_first(c, carry):
        for side in range(2):
            halo_copy(0, side, c).start()
        return carry

    lax.fori_loop(0, chunks, send_first, 0)

    lane = lax.broadcasted_iota(jnp.int32, (1, LANES), 1)
    first = lax.rem(lane, slot) < keep_x

    def swapped(values):
        return jnp.where(
            first, pltpu.roll(values, LANES - keep_x, 1), -pltpu.roll(values, keep_x, 1)
        )

    def transform(layer_of):
        pairs = jnp.concatenate(
            [
                jnp.concatenate([layer_of(2 * p), layer_of(2 * p + 1)], axis=1)
                for p in range(layers // 2)
            ],
            axis=0,
        )
        packed = times(pairs, xf)
        result = []
        for g in range(groups):
            total = None
            for p in range(slots // 2):
                index = g * (slots // 2) + p
                if index < layers // 2:
                    piece = packed[index * rows : (index + 1) * rows]
                    if p > 0:
                        piece = pltpu.roll(piece, 2 * p * slot, 1)
                    total = piece if total is None else total + piece
            result.append(total)
        both = [jnp.concatenate([t, swapped(t)], axis=0) for t in result]
        spec = under(yf, jnp.concatenate(both, axis=1))
        return jnp.concatenate([spec[:, g * LANES : (g + 1) * LANES] for g in range(groups)], axis=0)

    for copy in fills:
        copy.wait()

    own[...] = transform(lambda l: y1[l // depth, l % depth, pl.ds(PAD, rows)])
    ahead_copy = pltpu.make_async_remote_copy(
        src_ref=own,
        dst_ref=ahead,
        send_sem=ahead_sems.at[0],
        recv_sem=ahead_sems.at[1],
        device_id=(jnp.maximum(n - 1, 0), s),
        device_id_type=MESH,
    )

    @pl.when(n > 0)
    def _():
        ahead_copy.start()

    def update(stage, z, r0, below, above):
        state = states[stage]
        mid, xm, xp, ym, yp = [], [], [], [], []
        rolled = CHUNK + 2 * PAD
        for f in range(fields):
            wide = state[f, z, pl.ds(r0, rolled)]
            centre = wide[PAD : PAD + CHUNK]
            mid.append(centre)
            ym.append(pltpu.roll(wide, 1, 0)[PAD : PAD + CHUNK])
            yp.append(pltpu.roll(wide, rolled - 1, 0)[PAD : PAD + CHUNK])
            xm.append(pltpu.roll(centre, 1, 1))
            xp.append(pltpu.roll(centre, cols - 1, 1))
        zm = [below(f) for f in range(fields)]
        zp = [above(f) for f in range(fields)]
        sides = [xm, xp, ym, yp, zm, zp]
        factors = []
        for axis, speed in enumerate((advect_xaxis, advect_yaxis, advect_zaxis)):
            factors.append((viscosity + 0.5 * speed) + 0.5 * sides[2 * axis][axis])
            factors.append((viscosity - 0.5 * speed) - 0.5 * sides[2 * axis + 1][axis])
        shift = viscosity - diffusivity
        rates = []
        for f in range(fields):
            forcing = src[f, z, pl.ds(r0, CHUNK)]
            if f == 3:
                total = (
                    (xp[0] - xm[0]) + (yp[1] - ym[1]) + (zp[2] - zm[2])
                ) * (-0.5 * compress_rate)
            else:
                gain = viscosity if f < 3 else diffusivity
                total = (-6.0 * gain) * mid[f]
                for factor, side in zip(factors, sides):
                    total = total + (factor if f < 3 else factor - shift) * side[f]
                if f < 3:
                    total = total + 0.5 * (sides[2 * f][3] - sides[2 * f + 1][3])
            rates.append(total + forcing)
        share = time_step / 6.0 * (1.0, 2.0, 2.0, 1.0)[stage]
        for f in range(fields):
            at = f * depth + z
            here = pl.ds(r0, CHUNK)
            begin = y1[f, z, pl.ds(pl.multiple_of(r0 + PAD, 8), CHUNK)]
            done = begin if stage == 0 else fine[at, here]
            fine[at, here] = done + share * rates[f]
            if stage < 3:
                later = states[stage + 1]
                step = (0.5, 0.5, 1.0)[stage] * time_step
                value = begin + step * rates[f]
                later[f, z, pl.ds(pl.multiple_of(r0 + PAD, 8), CHUNK)] = value

                @pl.when(r0 == 0)
                def _():
                    later[f, z, pl.ds(PAD + rows, PAD)] = value[:PAD]

                @pl.when(r0 == rows - CHUNK)
                def _():
                    later[f, z, pl.ds(0, PAD)] = value[CHUNK - PAD :]

    for stage in range(4):
        state = states[stage]

        def inner(i, carry):
            z = 1 + i // chunks
            r0 = pl.multiple_of(lax.rem(i, chunks) * CHUNK, CHUNK)
            at = pl.ds(pl.multiple_of(r0 + PAD, 8), CHUNK)
            update(stage, z, r0, lambda f: state[f, z - 1, at], lambda f: state[f, z + 1, at])
            return carry

        def edge(c, carry):
            r0 = pl.multiple_of(c * CHUNK, CHUNK)
            at = pl.ds(pl.multiple_of(r0 + PAD, 8), CHUNK)
            for side in range(2):
                halo_copy(stage, side, c).wait_recv()
                here = lambda f: halo[stage, side, f, pl.ds(r0, CHUNK)]
                if side == 0:
                    update(stage, 0, r0, here, lambda f: state[f, 1, at])
                else:
                    update(stage, depth - 1, r0, lambda f: state[f, depth - 2, at], here)
                if stage < 3:
                    halo_copy(stage + 1, 1 - side, c).start()
            return carry

        lax.fori_loop(0, (depth - 2) * chunks, inner, 0)
        lax.fori_loop(0, chunks, edge, 0)

    spec = transform(lambda l: fine[l])

    @pl.when(n < times_n - 1)
    def _():
        ahead_copy.wait_recv()
        jumps[n] = spec - ahead[...]

    def jump_copy(slot_id, sem_id, target):
        return pltpu.make_async_remote_copy(
            src_ref=jumps.at[slot_id],
            dst_ref=jumps.at[slot_id],
            send_sem=jump_send.at[sem_id],
            recv_sem=jump_recv.at[slot_id],
            device_id=(target, s),
            device_id_type=MESH,
        )

    def send_jump(i, carry):
        target = times_n - 1 - i
        jump_copy(n, target, target).start()
        return carry

    lax.fori_loop(0, times_n - 1 - n, send_jump, 0)

    width = depth * spaces * keep_x
    gain_re = jnp.concatenate([sym[0]] * groups, axis=0)
    gain_im = jnp.concatenate([sym[1]] * groups, axis=0)

    def advance(carry):
        result = []
        for p in range(per):
            re, im = carry[2 * p], carry[2 * p + 1]
            result.append(gain_re * re - gain_im * im)
            result.append(gain_re * im + gain_im * re)
        return result

    def collect(m, carry):
        jump_copy(m, m, n).wait_recv()
        fresh = times(jumps[m], zf)
        return tuple(
            a + fresh[:, i * width : (i + 1) * width] for i, a in enumerate(advance(carry))
        )

    zero = jnp.zeros((groups * ky, width), jnp.float32)
    carry = advance(lax.fori_loop(0, n, collect, (zero,) * (2 * per)))
    stacked = jnp.concatenate(
        [jnp.concatenate([carry[2 * p], carry[2 * p + 1]], axis=1) for p in range(per)], axis=0
    )
    back = times(stacked, zi)
    half = depth * slot
    height = groups * ky

    def piece(offset):
        total = None
        at = offset * half
        tile, inside = at // LANES * LANES, at % LANES
        part = lax.broadcasted_iota(jnp.int32, (1, LANES), 1) // half
        for p in range(per):
            block = back[p * height : (p + 1) * height, tile : tile + LANES]
            move = (p * half - inside) % LANES
            if move:
                block = pltpu.roll(block, move, 1)
            total = block if total is None else jnp.where(part == p, block, total)
        return total

    def mode_copy(offset):
        return pltpu.make_async_remote_copy(
            src_ref=mode_send.at[offset - 1],
            dst_ref=mode_recv.at[offset - 1],
            send_sem=mode_ssem.at[offset - 1],
            recv_sem=mode_rsem.at[offset - 1],
            device_id=(n, lax.rem(s + offset, spaces)),
            device_id_type=MESH,
        )

    for offset in range(1, spaces):
        mode_send[offset - 1] = piece(offset)
        mode_copy(offset).start()
    modes = piece(0)
    for offset in range(1, spaces):
        mode_copy(offset).wait_recv()
        modes = modes + mode_recv[offset - 1]

    weight = jnp.where(lax.rem(lane, keep_x) == 0, 1.0, 2.0)
    scaled = modes * (1.0 / (depth * spaces * rows * cols))
    square = jnp.sum(
        jnp.sum(scaled * scaled * weight, axis=0, keepdims=True), axis=1, keepdims=True
    ) * float(rows * cols)
    square_send[...] = jnp.broadcast_to(square, (1, LANES))
    squares[me] = jnp.broadcast_to(square, (1, LANES))

    def square_copy(index, target):
        return pltpu.make_async_remote_copy(
            src_ref=square_send,
            dst_ref=squares.at[index],
            send_sem=sq_send.at[target],
            recv_sem=sq_recv.at[index],
            device_id=(target // spaces, lax.rem(target, spaces)),
            device_id_type=MESH,
        )

    def send_square(i, carry):
        @pl.when(i != me)
        def _():
            square_copy(me, i).start()

        return carry

    lax.fori_loop(0, devices, send_square, 0)

    both = [
        jnp.concatenate([t, swapped(t)], axis=0)
        for t in (modes[g * ky : (g + 1) * ky] for g in range(groups))
    ]
    planes = under(yi, jnp.concatenate(both, axis=1))
    outs = []
    for g in range(groups):
        plane = planes[:, g * LANES : (g + 1) * LANES]
        count = min(slots, layers - g * slots) // 2
        shifted = [
            plane if p == 0 else pltpu.roll(plane, LANES - 2 * p * slot, 1) for p in range(count)
        ]
        fix = times(jnp.concatenate(shifted, axis=0), xi)
        for p in range(count):
            for i in range(2):
                l = g * slots + 2 * p + i
                fine[l] = fine[l] + fix[p * rows : (p + 1) * rows, i * cols : (i + 1) * cols]
        low = g * slots // depth
        held = 2 * count // depth
        for f in range(low, low + held):
            copy = pltpu.make_async_copy(
                fine.at[pl.ds(f * depth, depth)], ends.at[0, f], out_sem.at[f]
            )
            copy.start()
            outs.append(copy)

    def take_square(i, carry):
        @pl.when(i != me)
        def _():
            square_copy(i, i).wait_recv()

        return carry

    lax.fori_loop(0, devices, take_square, 0)
    cells = fields * depth * spaces * rows * cols
    mine = jnp.sum(squares[pl.ds(n * spaces, spaces)], axis=0)
    every = jnp.sum(squares[...], axis=0)
    slice_out[...] = jnp.sqrt(mine * (1.0 / cells) + epsilon)
    total_out[...] = jnp.sqrt(every * (1.0 / (cells * times_n)) + epsilon)

    def drain_square(i, carry):
        @pl.when(i != me)
        def _():
            square_copy(me, i).wait_send()

        return carry

    lax.fori_loop(0, devices, drain_square, 0)

    def drain_jump(i, carry):
        target = times_n - 1 - i
        jump_copy(n, target, target).wait_send()
        return carry

    lax.fori_loop(0, times_n - 1 - n, drain_jump, 0)

    @pl.when(n > 0)
    def _():
        ahead_copy.wait_send()

    for stage in range(4):

        def drain_halo(c, carry):
            for side in range(2):
                halo_copy(stage, side, c).wait_send()
            return carry

        lax.fori_loop(0, chunks, drain_halo, 0)
    for offset in range(1, spaces):
        mode_copy(offset).wait_send()
    for copy in outs:
        copy.wait()


def solution(mesh):
    times_n, spaces = mesh.shape["tm"], mesh.shape["space"]

    def step(starts, source):
        _, fields, depth, rows, cols = starts.shape
        keep_y, keep_x = rows // 8, cols // 16
        matrices, symbol = tables(depth, rows, cols, spaces)
        constants = [halves(t) for t in matrices] + [symbol]
        ky, slot = 2 * keep_y, 2 * keep_x
        groups = -(-fields * depth // (LANES // slot))
        height = groups * ky
        devices = times_n * spaces
        chunks = rows // CHUNK
        state = pltpu.VMEM((fields, depth, rows + 2 * PAD, cols), jnp.float32)
        dma = pltpu.SemaphoreType.DMA
        ends, slice_row, total_row = pl.pallas_call(
            functools.partial(kernel, (times_n, spaces, fields, depth, rows, cols)),
            out_shape=(
                jax.ShapeDtypeStruct(starts.shape, jnp.float32),
                jax.ShapeDtypeStruct((1, LANES), jnp.float32),
                jax.ShapeDtypeStruct((1, LANES), jnp.float32),
            ),
            in_specs=[pl.BlockSpec(memory_space=pl.ANY)] * (2 + len(constants)),
            out_specs=(
                pl.BlockSpec(memory_space=pl.ANY),
                pl.BlockSpec(memory_space=pltpu.VMEM),
                pl.BlockSpec(memory_space=pltpu.VMEM),
            ),
            scratch_shapes=[
                state, state, state, state,
                pltpu.VMEM((fields, depth, rows, cols), jnp.float32),
                pltpu.VMEM((fields * depth, rows, cols), jnp.float32),
                pltpu.VMEM((4, 2, fields, rows, cols), jnp.float32),
                *[pltpu.VMEM(c.shape, c.dtype) for c in constants],
                pltpu.VMEM((height, LANES), jnp.float32),
                pltpu.VMEM((times_n, height, LANES), jnp.float32),
                pltpu.VMEM((height, LANES), jnp.float32),
                pltpu.VMEM((spaces - 1, height, LANES), jnp.float32),
                pltpu.VMEM((spaces - 1, height, LANES), jnp.float32),
                pltpu.VMEM((1, LANES), jnp.float32),
                pltpu.VMEM((devices, 1, LANES), jnp.float32),
                dma((4,)), dma((len(constants),)),
                dma((4, 2, chunks)), dma((4, 2, chunks)), dma((2,)),
                dma((times_n,)), dma((times_n,)),
                dma((spaces - 1,)), dma((spaces - 1,)),
                dma((devices,)), dma((devices,)), dma((fields,)),
            ],
            compiler_params=pltpu.CompilerParams(
                collective_id=0, has_side_effects=True, vmem_limit_bytes=48 * 1024 * 1024
            ),
        )(starts, source, *[jnp.asarray(c) for c in constants])
        return ends, slice_row[0, :1], total_row[0, :1]

    return jax.shard_map(
        step,
        mesh=mesh,
        in_specs=(P("tm", None, "space", None, None), P(None, "space", None, None)),
        out_specs=(P("tm", None, "space", None, None), P("tm"), P()),
        check_vma=False,
    )
```

time: 203 us -> 52.1 us (0.26)
  blocking collectives: 65.3 us -> 0 us
  waiting for transfers between devices: 45.6 us -> 0 us
  Pallas kernels: 0 us -> 39.8 us
  matrix products: 24.5 us -> 0 us
  between operations: 19.9 us -> 2.98 us
  other arithmetic: 16 us -> 0 us
  local copies, waits for them, and re-layouts: 22.2 us -> 8.88 us
  starting transfers between devices: 8.72 us -> 0 us
    pallas_call x0 -> x1, Pallas kernels: none -> 39.8 us  [step(): pl.pallas_call(functools.partial(kernel, (times_n, spaces, fields, depth,...]
    all_gather x2 -> x0, blocking collectives: 36.8 us -> none  [the longest x1 31.1 us: shards(): portion = lax.all_gather(jumps[None], 'tm', axis=0, tiled=True)]
    unnamed x2 -> x0, waiting for transfers between devices: 32.7 us -> none
    psum x2 -> x0, blocking collectives: 28.5 us -> none  [the longest x1 21.8 us: shards(): every_sum = lax.psum(slice_sum, 'tm')]
    dot_general x20 -> x0, matrix products: 24.5 us -> none  [the longest x1 3.22 us: shards(): imag_x = -jnp.einsum('bzyx,xk->bzyk', stacked, xsines, precision=highest)]
    ppermute x8 -> x0, waiting for transfers between devices: 12.8 us -> none  [the longest x4 8.68 us: with_halo(): lax.ppermute(tail, axis, [(i, (i + 1) % count) for i in range(count)])]
    slice x125 -> x0, local copies, waits for them, and re-layouts: 11.9 us -> none  [the longest x42 4.51 us: laplace(): summed = summed + jnp.roll(interior, -1, axis) + jnp.roll(interior, 1, axis)]
    ppermute x8 -> x0, starting transfers between devices: 8.69 us -> none  [the longest x4 5.7 us: with_halo(): lax.ppermute(head, axis, [((i + 1) % count, i) for i in range(count)])]
  transfers between devices with their start and end apart: 9 -> 0, of which waited for: 7 -> 0; matrix products, arithmetic and copies ran while one was open for 7% -> 0% of each run, Pallas kernels for 0% -> 0%
where the time goes in v1:
time: 52.1 us; the launch traced here: 51.6 us
  Pallas kernels  39.8 us (76%)
  local copies, waits for them, and re-layouts  8.88 us (17%)
  between operations  2.98 us (6%)
    pallas_call x1, Pallas kernels, step(): pl.pallas_call(functools.partial(kernel, (times_n, spaces, fields, depth,...  39.8 us
    unnamed x19, local copies, waits for them, and re-layouts  8.88 us

profile of v1, /device:TPU:0, one launch (start us, length us, event | category | flops | bytes accessed | tf_op | source)
XLA Modules:
  0.0 51.6 jit_solution(7851859744615440689)
XLA Ops:
  0.6 0.0 copy-start
  0.6 1.1 %copy-done = f32[1,5,4,64,128]{4,3,2,1,0:T(8,128)S(1)} copy-done((f32[1,5,4,64,128]{4,3,2,1,0:T(8,128)S(1)}, f32[1,5,4,64,128]{4,3,2,1,0:T(8,128)}, u32[]{:S(2)}) %copy-start) | copy-done | bytes 655384
  1.7 0.0 copy-start.1
  1.7 1.1 %copy-done.1 = f32[5,4,64,128]{3,2,1,0:T(8,128)S(1)} copy-done((f32[5,4,64,128]{3,2,1,0:T(8,128)S(1)}, f32[5,4,64,128]{3,2,1,0:T(8,128)}, u32[]{:S(2)}) %copy-start.1) | copy-done | bytes 655384
  2.8 0.0 copy-start.2
  2.8 0.9 %copy-done.2 = bf16[2,256,256]{2,1,0:T(8,128)(2,1)S(1)} copy-done((bf16[2,256,256]{2,1,0:T(8,128)(2,1)S(1)}, bf16[2,256,256]{2,1,0:T(8,128)(2,1)}, u32[]{:S(2)}) %copy-start.2) | copy-done | bytes 262168
  3.8 0.0 copy-start.3
  3.8 0.9 %copy-done.3 = bf16[2,128,512]{2,1,0:T(8,128)(2,1)S(1)} copy-done((bf16[2,128,512]{2,1,0:T(8,128)(2,1)S(1)}, bf16[2,128,512]{2,1,0:T(8,128)(2,1)}, u32[]{:S(2)}) %copy-start.3) | copy-done | bytes 262168
  4.7 0.0 copy-start.4
  4.7 0.9 %copy-done.4 = bf16[2,128,256]{2,1,0:T(8,128)(2,1)S(1)} copy-done((bf16[2,128,256]{2,1,0:T(8,128)(2,1)S(1)}, bf16[2,128,256]{2,1,0:T(8,128)(2,1)}, u32[]{:S(2)}) %copy-start.4) | copy-done | bytes 131096
  5.6 0.0 copy-start.5
  5.6 0.9 %copy-done.5 = bf16[2,256,128]{2,1,0:T(8,128)(2,1)S(1)} copy-done((bf16[2,256,128]{2,1,0:T(8,128)(2,1)S(1)}, bf16[2,256,128]{2,1,0:T(8,128)(2,1)}, u32[]{:S(2)}) %copy-start.5) | copy-done | bytes 131096
  6.5 0.0 copy-start.6
  6.5 0.8 %copy-done.6 = bf16[2,64,32]{2,1,0:T(8,128)(2,1)S(1)} copy-done((bf16[2,64,32]{2,1,0:T(8,128)(2,1)S(1)}, bf16[2,64,32]{2,1,0:T(8,128)(2,1)}, u32[]{:S(2)}) %copy-start.6) | copy-done | bytes 8216
  7.3 0.0 copy-start.7
  7.3 0.7 %copy-done.7 = f32[2,16,128]{2,1,0:T(8,128)S(1)} copy-done((f32[2,16,128]{2,1,0:T(8,128)S(1)}, f32[2,16,128]{2,1,0:T(8,128)}, u32[]{:S(2)}) %copy-start.7) | copy-done | bytes 16408
  8.0 0.0 copy-start.8
  8.0 0.7 %copy-done.8 = bf16[2,16,128]{2,1,0:T(8,128)(2,1)S(1)} copy-done((bf16[2,16,128]{2,1,0:T(8,128)(2,1)S(1)}, bf16[2,16,128]{2,1,0:T(8,128)(2,1)}, u32[]{:S(2)}) %copy-start.8) | copy-done | bytes 8216
  8.7 39.8 %shard_map.112 = (f32[1,5,4,64,128]{4,3,2,1,0:T(8,128)S(1)}, f32[1,128]{1,0:T(1,128)S(1)}, f32[1,128]{1,0:T(1,128)S(1)}) custom-call(f32[1,5,4,64,128]{4,3,2,1,0:T(8,128)S(1)} %copy-done, f32[5,4,64,128]{3,2,1,0:T(8,128)S(1)} %copy-done.1, bf16[2,256,128]{2,1,0:T(8,128)(2,1)S(1)} %copy-done.5, bf16[2,16,128]{2,1,0:T(8,128)(2,1)S(1)} %copy-done.8, ...), custom_call_target="tpu_custom_call" | custom-call | tf_op jit(solution)/shard_map/pallas_call | solution.py:532
  48.5 0.8 %copy.15 = f32[1,5,4,64,128]{4,3,2,1,0:T(8,128)} copy(f32[1,5,4,64,128]{4,3,2,1,0:T(8,128)S(1)} %get-tuple-element.12) | data formatting | bytes 1310720
Async XLA Ops:
  0.6 1.1 %copy-start = (f32[1,5,4,64,128]{4,3,2,1,0:T(8,128)S(1)}, f32[1,5,4,64,128]{4,3,2,1,0:T(8,128)}, u32[]{:S(2)}) copy-start(f32[1,5,4,64,128]{4,3,2,1,0:T(8,128)} %starts.1) | copy-start | bytes 1966084
  1.7 1.1 %copy-start.1 = (f32[5,4,64,128]{3,2,1,0:T(8,128)S(1)}, f32[5,4,64,128]{3,2,1,0:T(8,128)}, u32[]{:S(2)}) copy-start(f32[5,4,64,128]{3,2,1,0:T(8,128)} %source.1) | copy-start | bytes 1966084
  2.8 0.9 %copy-start.2 = (bf16[2,256,256]{2,1,0:T(8,128)(2,1)S(1)}, bf16[2,256,256]{2,1,0:T(8,128)(2,1)}, u32[]{:S(2)}) copy-start(bf16[2,256,256]{2,1,0:T(8,128)(2,1)} %constant.17.clone.zi_h) | copy-start | bytes 786436
  3.8 0.9 %copy-start.3 = (bf16[2,128,512]{2,1,0:T(8,128)(2,1)S(1)}, bf16[2,128,512]{2,1,0:T(8,128)(2,1)}, u32[]{:S(2)}) copy-start(bf16[2,128,512]{2,1,0:T(8,128)(2,1)} %constant.16.clone.zf_h) | copy-start | bytes 786436
  4.7 0.9 %copy-start.4 = (bf16[2,128,256]{2,1,0:T(8,128)(2,1)S(1)}, bf16[2,128,256]{2,1,0:T(8,128)(2,1)}, u32[]{:S(2)}) copy-start(bf16[2,128,256]{2,1,0:T(8,128)(2,1)} %constant.19.clone.xi_h) | copy-start | bytes 393220
  5.6 0.9 %copy-start.5 = (bf16[2,256,128]{2,1,0:T(8,128)(2,1)S(1)}, bf16[2,256,128]{2,1,0:T(8,128)(2,1)}, u32[]{:S(2)}) copy-start(bf16[2,256,128]{2,1,0:T(8,128)(2,1)} %constant.14.clone.xf_h) | copy-start | bytes 393220
  6.5 0.8 %copy-start.6 = (bf16[2,64,32]{2,1,0:T(8,128)(2,1)S(1)}, bf16[2,64,32]{2,1,0:T(8,128)(2,1)}, u32[]{:S(2)}) copy-start(bf16[2,64,32]{2,1,0:T(8,128)(2,1)} %constant.18.clone.yi_h) | copy-start | bytes 24580
  7.3 0.7 %copy-start.7 = (f32[2,16,128]{2,1,0:T(8,128)S(1)}, f32[2,16,128]{2,1,0:T(8,128)}, u32[]{:S(2)}) copy-start(f32[2,16,128]{2,1,0:T(8,128)} %constant.20.clone.sym_h) | copy-start | bytes 49156
  8.0 0.7 %copy-start.8 = (bf16[2,16,128]{2,1,0:T(8,128)(2,1)S(1)}, bf16[2,16,128]{2,1,0:T(8,128)(2,1)}, u32[]{:S(2)}) copy-start(bf16[2,16,128]{2,1,0:T(8,128)(2,1)} %constant.15.clone.yf_h) | copy-start | bytes 24580

commit v2 on v1

--- a/solution.py
+++ b/solution.py
@@ -24,7 +24,7 @@
 LANES = 128
 
 
-def tables(depth, rows, cols, spaces):
+def tables(depth, rows, cols, spaces, steps):
     keep_y, keep_x = rows // 8, cols // 16
     slot = 2 * keep_x
     per = LANES // (slot * depth)
@@ -87,8 +87,10 @@
         + advect_zaxis * np.sin(tz)[None, :, None]
         + advect_xaxis * np.sin(tx)[None, None, :]
     )
-    symbol = np.stack([real * live, imag * live]).reshape(2, 2 * keep_y, width)
-    return [xf, yf, zf, zi, yi, xi], symbol.astype(np.float32)
+    symbol = (real + 1j * imag) * live
+    powers = np.stack([symbol**p for p in range(1, max(steps, 2))])
+    powers = np.stack([powers.real, powers.imag], axis=1).reshape(-1, 2, 2 * keep_y, width)
+    return [xf, yf, zf, zi, yi, xi], powers.astype(np.float32)
 
 
 def halves(table):
@@ -118,11 +120,11 @@
 
 def kernel(
     sizes, starts, source, xf_h, yf_h, zf_h, zi_h, yi_h, xi_h, sym_h,
-    ends, slice_out, total_out,
-    y1, y2, y3, y4, src, fine, halo, xf, yf, zf, zi, yi, xi, sym,
+    fine_out, fix_out, slice_out, total_out,
+    y1, y2, y3, y4, src, fine, fixes, halo, xf, yf, zf, zi, yi, xi, sym,
     own, jumps, ahead, mode_send, mode_recv, square_send, squares,
     load_sem, table_sem, halo_send, halo_recv, ahead_sems, jump_send, jump_recv,
-    mode_ssem, mode_rsem, sq_send, sq_recv, out_sem,
+    mode_ssem, mode_rsem, sq_send, sq_recv, out_sem, relays,
 ):
     times_n, spaces, fields, depth, rows, cols = sizes
     keep_y, keep_x = rows // 8, cols // 16
@@ -133,7 +135,6 @@
     groups = -(-layers // slots)
     per = LANES // (slot * depth)
     chunks = rows // CHUNK
-    devices = times_n * spaces
     n = lax.axis_index("tm")
     s = lax.axis_index("space")
     me = n * spaces + s
@@ -142,18 +143,26 @@
 
     barrier = pltpu.get_barrier_semaphore()
 
-    def greet(i, c):
-        @pl.when(i != me)
-        def _():
-            pl.semaphore_signal(
-                barrier, inc=1, device_id=(i // spaces, lax.rem(i, spaces)), device_id_type=MESH
-            )
-
-        return c
-
-    lax.fori_loop(0, devices, greet, 0)
+    def near(distance, act):
+        for side, target in enumerate((n - distance, n + distance)):
+            pl.when((target >= 0) & (target < times_n))(functools.partial(act, side, target))
+
+    def enter(target, where):
+        pl.semaphore_signal(barrier, inc=1, device_id=(target, where), device_id_type=MESH)
+
+    for offset in range(1, spaces):
+        enter(n, lax.rem(s + offset, spaces))
+    near(1, lambda side, target: enter(target, s))
     loads = [
-        pltpu.make_async_copy(starts.at[0], y1.at[:, :, pl.ds(PAD, rows)], load_sem.at[0]),
+        pltpu.make_async_copy(starts.at[0, :, 0], y1.at[:, 0, pl.ds(PAD, rows)], load_sem.at[0]),
+        pltpu.make_async_copy(
+            starts.at[0, :, depth - 1], y1.at[:, depth - 1, pl.ds(PAD, rows)], load_sem.at[4]
+        ),
+        pltpu.make_async_copy(
+            starts.at[0, :, pl.ds(1, depth - 2)],
+            y1.at[:, pl.ds(1, depth - 2), pl.ds(PAD, rows)],
+            load_sem.at[5],
+        ),
         pltpu.make_async_copy(
             starts.at[0, :, :, pl.ds(rows - PAD, PAD)], y1.at[:, :, pl.ds(0, PAD)], load_sem.at[1]
         ),
@@ -172,9 +181,23 @@
     ]
     for copy in fills:
         copy.start()
-    for copy in loads:
+    for copy in loads[:2]:
         copy.wait()
-    pl.semaphore_wait(barrier, devices - 1)
+    beside = jnp.where(n > 0, 1, 0) + jnp.where(n < times_n - 1, 1, 0)
+    pl.semaphore_wait(barrier, spaces - 1 + beside)
+
+    def relay(level):
+        near(
+            2**level,
+            lambda side, target: pl.semaphore_signal(
+                relays.at[level, side], inc=1, device_id=(target, s), device_id_type=MESH
+            ),
+        )
+
+    def heard(level):
+        near(2**level, lambda side, target: pl.semaphore_wait(relays.at[level, 1 - side], 1))
+
+    levels = (times_n - 1).bit_length()
 
     states = [y1, y2, y3, y4]
 
@@ -197,6 +220,7 @@
         return carry
 
     lax.fori_loop(0, chunks, send_first, 0)
+    relay(0)
 
     lane = lax.broadcasted_iota(jnp.int32, (1, LANES), 1)
     first = lax.rem(lane, slot) < keep_x
@@ -230,7 +254,7 @@
         spec = under(yf, jnp.concatenate(both, axis=1))
         return jnp.concatenate([spec[:, g * LANES : (g + 1) * LANES] for g in range(groups)], axis=0)
 
-    for copy in fills:
+    for copy in loads[2:] + fills:
         copy.wait()
 
     own[...] = transform(lambda l: y1[l // depth, l % depth, pl.ds(PAD, rows)])
@@ -329,7 +353,14 @@
 
         lax.fori_loop(0, (depth - 2) * chunks, inner, 0)
         lax.fori_loop(0, chunks, edge, 0)
-
+        for level in range(levels):
+            if min(level, 2) == stage:
+                heard(level)
+                if level + 1 < levels:
+                    relay(level + 1)
+
+    outs = [pltpu.make_async_copy(fine, fine_out, out_sem.at[0])]
+    outs[0].start()
     spec = transform(lambda l: fine[l])
 
     @pl.when(n < times_n - 1)
@@ -355,26 +386,23 @@
     lax.fori_loop(0, times_n - 1 - n, send_jump, 0)
 
     width = depth * spaces * keep_x
-    gain_re = jnp.concatenate([sym[0]] * groups, axis=0)
-    gain_im = jnp.concatenate([sym[1]] * groups, axis=0)
-
-    def advance(carry):
+
+    def collect(i, carry):
+        m = n - 1 - i
+        jump_copy(m, m, n).wait_recv()
+        fresh = times(jumps[m], zf)
+        gain_re = jnp.concatenate([sym[i, 0]] * groups, axis=0)
+        gain_im = jnp.concatenate([sym[i, 1]] * groups, axis=0)
         result = []
         for p in range(per):
-            re, im = carry[2 * p], carry[2 * p + 1]
-            result.append(gain_re * re - gain_im * im)
-            result.append(gain_re * im + gain_im * re)
-        return result
-
-    def collect(m, carry):
-        jump_copy(m, m, n).wait_recv()
-        fresh = times(jumps[m], zf)
-        return tuple(
-            a + fresh[:, i * width : (i + 1) * width] for i, a in enumerate(advance(carry))
-        )
+            re = fresh[:, 2 * p * width : (2 * p + 1) * width]
+            im = fresh[:, (2 * p + 1) * width : (2 * p + 2) * width]
+            result.append(carry[2 * p] + (gain_re * re - gain_im * im))
+            result.append(carry[2 * p + 1] + (gain_re * im + gain_im * re))
+        return tuple(result)
 
     zero = jnp.zeros((groups * ky, width), jnp.float32)
-    carry = advance(lax.fori_loop(0, n, collect, (zero,) * (2 * per)))
+    carry = lax.fori_loop(0, n, collect, (zero,) * (2 * per))
     stacked = jnp.concatenate(
         [jnp.concatenate([carry[2 * p], carry[2 * p + 1]], axis=1) for p in range(per)], axis=0
     )
@@ -421,31 +449,43 @@
     square_send[...] = jnp.broadcast_to(square, (1, LANES))
     squares[me] = jnp.broadcast_to(square, (1, LANES))
 
-    def square_copy(index, target):
+    def square_copy(index, sem_id, target):
         return pltpu.make_async_remote_copy(
             src_ref=square_send,
             dst_ref=squares.at[index],
-            send_sem=sq_send.at[target],
+            send_sem=sq_send.at[sem_id],
             recv_sem=sq_recv.at[index],
-            device_id=(target // spaces, lax.rem(target, spaces)),
+            device_id=target,
             device_id_type=MESH,
         )
 
-    def send_square(i, carry):
-        @pl.when(i != me)
-        def _():
-            square_copy(me, i).start()
-
-        return carry
-
-    lax.fori_loop(0, devices, send_square, 0)
+    def others(act):
+        def body(dt, carry):
+            t = n - dt
+            t = jnp.where(t < 0, t + times_n, t)
+            for ds in range(spaces):
+                where = s + ds
+                where = jnp.where(where >= spaces, where - spaces, where)
+                run = functools.partial(act, dt * spaces + ds, t, where)
+                if ds == 0:
+                    pl.when(dt > 0)(run)
+                else:
+                    run()
+            return carry
+
+        if times_n <= 8:
+            for dt in range(times_n):
+                body(dt, 0)
+        else:
+            lax.fori_loop(0, times_n, body, 0)
+
+    others(lambda k, t, where: square_copy(me, k, (t, where)).start())
 
     both = [
         jnp.concatenate([t, swapped(t)], axis=0)
         for t in (modes[g * ky : (g + 1) * ky] for g in range(groups))
     ]
     planes = under(yi, jnp.concatenate(both, axis=1))
-    outs = []
     for g in range(groups):
         plane = planes[:, g * LANES : (g + 1) * LANES]
         count = min(slots, layers - g * slots) // 2
@@ -456,38 +496,22 @@
         for p in range(count):
             for i in range(2):
                 l = g * slots + 2 * p + i
-                fine[l] = fine[l] + fix[p * rows : (p + 1) * rows, i * cols : (i + 1) * cols]
-        low = g * slots // depth
-        held = 2 * count // depth
-        for f in range(low, low + held):
-            copy = pltpu.make_async_copy(
-                fine.at[pl.ds(f * depth, depth)], ends.at[0, f], out_sem.at[f]
-            )
-            copy.start()
-            outs.append(copy)
-
-    def take_square(i, carry):
-        @pl.when(i != me)
-        def _():
-            square_copy(i, i).wait_recv()
-
-        return carry
-
-    lax.fori_loop(0, devices, take_square, 0)
+                fixes[l] = fix[p * rows : (p + 1) * rows, i * cols : (i + 1) * cols]
+        held = pl.ds(g * slots, 2 * count)
+        copy = pltpu.make_async_copy(fixes.at[held], fix_out.at[held], out_sem.at[1 + g])
+        copy.start()
+        outs.append(copy)
+
+    others(
+        lambda k, t, where: square_copy(t * spaces + where, k, (t, where)).wait_recv()
+    )
     cells = fields * depth * spaces * rows * cols
     mine = jnp.sum(squares[pl.ds(n * spaces, spaces)], axis=0)
     every = jnp.sum(squares[...], axis=0)
-    slice_out[...] = jnp.sqrt(mine * (1.0 / cells) + epsilon)
-    total_out[...] = jnp.sqrt(every * (1.0 / (cells * times_n)) + epsilon)
-
-    def drain_square(i, carry):
-        @pl.when(i != me)
-        def _():
-            square_copy(me, i).wait_send()
-
-        return carry
-
-    lax.fori_loop(0, devices, drain_square, 0)
+    slice_out[0] = jnp.sqrt(mine * (1.0 / cells) + epsilon)[0, 0]
+    total_out[0] = jnp.sqrt(every * (1.0 / (cells * times_n)) + epsilon)[0, 0]
+
+    others(lambda k, t, where: square_copy(me, k, (t, where)).wait_send())
 
     def drain_jump(i, carry):
         target = times_n - 1 - i
@@ -520,32 +544,36 @@
     def step(starts, source):
         _, fields, depth, rows, cols = starts.shape
         keep_y, keep_x = rows // 8, cols // 16
-        matrices, symbol = tables(depth, rows, cols, spaces)
+        matrices, symbol = tables(depth, rows, cols, spaces, times_n)
         constants = [halves(t) for t in matrices] + [symbol]
         ky, slot = 2 * keep_y, 2 * keep_x
         groups = -(-fields * depth // (LANES // slot))
         height = groups * ky
+        chunks = rows // CHUNK
         devices = times_n * spaces
-        chunks = rows // CHUNK
         state = pltpu.VMEM((fields, depth, rows + 2 * PAD, cols), jnp.float32)
         dma = pltpu.SemaphoreType.DMA
-        ends, slice_row, total_row = pl.pallas_call(
+        layer_shape = (fields * depth, rows, cols)
+        fine, fix, slice_norm, total_norm = pl.pallas_call(
             functools.partial(kernel, (times_n, spaces, fields, depth, rows, cols)),
             out_shape=(
-                jax.ShapeDtypeStruct(starts.shape, jnp.float32),
-                jax.ShapeDtypeStruct((1, LANES), jnp.float32),
-                jax.ShapeDtypeStruct((1, LANES), jnp.float32),
+                jax.ShapeDtypeStruct(layer_shape, jnp.float32),
+                jax.ShapeDtypeStruct(layer_shape, jnp.float32),
+                jax.ShapeDtypeStruct((1,), jnp.float32),
+                jax.ShapeDtypeStruct((1,), jnp.float32),
             ),
-            in_specs=[pl.BlockSpec(memory_space=pl.ANY)] * (2 + len(constants)),
+            in_specs=[pl.BlockSpec(memory_space=pltpu.HBM)] * (2 + len(constants)),
             out_specs=(
                 pl.BlockSpec(memory_space=pl.ANY),
-                pl.BlockSpec(memory_space=pltpu.VMEM),
-                pl.BlockSpec(memory_space=pltpu.VMEM),
+                pl.BlockSpec(memory_space=pl.ANY),
+                pl.BlockSpec(memory_space=pltpu.SMEM),
+                pl.BlockSpec(memory_space=pltpu.SMEM),
             ),
             scratch_shapes=[
                 state, state, state, state,
                 pltpu.VMEM((fields, depth, rows, cols), jnp.float32),
-                pltpu.VMEM((fields * depth, rows, cols), jnp.float32),
+                pltpu.VMEM(layer_shape, jnp.float32),
+                pltpu.VMEM(layer_shape, jnp.float32),
                 pltpu.VMEM((4, 2, fields, rows, cols), jnp.float32),
                 *[pltpu.VMEM(c.shape, c.dtype) for c in constants],
                 pltpu.VMEM((height, LANES), jnp.float32),
@@ -555,17 +583,18 @@
                 pltpu.VMEM((spaces - 1, height, LANES), jnp.float32),
                 pltpu.VMEM((1, LANES), jnp.float32),
                 pltpu.VMEM((devices, 1, LANES), jnp.float32),
-                dma((4,)), dma((len(constants),)),
+                dma((6,)), dma((len(constants),)),
                 dma((4, 2, chunks)), dma((4, 2, chunks)), dma((2,)),
                 dma((times_n,)), dma((times_n,)),
                 dma((spaces - 1,)), dma((spaces - 1,)),
-                dma((devices,)), dma((devices,)), dma((fields,)),
+                dma((devices,)), dma((devices,)), dma((2 * fields,)),
+                pltpu.SemaphoreType.REGULAR(((times_n - 1).bit_length(), 2)),
             ],
             compiler_params=pltpu.CompilerParams(
-                collective_id=0, has_side_effects=True, vmem_limit_bytes=48 * 1024 * 1024
+                collective_id=0, has_side_effects=True, vmem_limit_bytes=67043328
             ),
         )(starts, source, *[jnp.asarray(c) for c in constants])
-        return ends, slice_row[0, :1], total_row[0, :1]
+        return (fine + fix).reshape(starts.shape), slice_norm, total_norm
 
     return jax.shard_map(
         step,

time: 52.1 us -> 44.1 us (0.85)
  local copies, waits for them, and re-layouts: 8.88 us -> 0 us
  Pallas kernels: 39.8 us -> 37.5 us
  other arithmetic: 0 us -> 2.21 us
  between operations: 2.98 us -> 4.2 us
    unnamed x19 -> x0, local copies, waits for them, and re-layouts: 8.88 us -> none
    pallas_call x1, Pallas kernels: 39.8 us -> 37.5 us  [step(): pl.pallas_call(functools.partial(kernel, (times_n, spaces, fields, depth,...]
    add x0 -> x1, other arithmetic: none -> 2.21 us  [step(): return ((fine + fix).reshape(starts.shape), slice_norm, total_norm)]
where the time goes in v2:
time: 44.1 us; the launch traced here: 43.9 us
  Pallas kernels  37.5 us (85%)
  between operations  4.2 us (10%)
  other arithmetic  2.21 us (5%)
    pallas_call x1, Pallas kernels, step(): pl.pallas_call(functools.partial(kernel, (times_n, spaces, fields, depth,...  37.5 us
    add x1, other arithmetic, step(): return ((fine + fix).reshape(starts.shape), slice_norm, total_norm)  2.21 us

profile of v2, /device:TPU:0, one launch (start us, length us, event | category | flops | bytes accessed | tf_op | source)
XLA Modules:
  0.0 43.9 jit_solution(709130385524806727)
XLA Ops:
  0.6 37.5 %shard_map.112 = (f32[20,64,128]{2,1,0:T(8,128)}, f32[20,64,128]{2,1,0:T(8,128)}, f32[1]{0:T(128)}, f32[1]{0:T(128)}) custom-call(f32[1,5,4,64,128]{4,3,2,1,0:T(8,128)} %starts.1, f32[5,4,64,128]{3,2,1,0:T(8,128)} %source.1, bf16[2,256,128]{2,1,0:T(8,128)(2,1)} %constant.14.clone.xf_h, bf16[2,16,128]{2,1,0:T(8,128)(2,1)} %constant.15.clone.yf_h, ...), custom_call_target="tpu_custom_call" | custom-call | tf_op jit(solution)/shard_map/pallas_call | solution.py:557
  38.2 2.2 %add.3 = f32[20,64,128]{2,1,0:T(8,128)} add(f32[20,64,128]{2,1,0:T(8,128)} %get-tuple-element.7, f32[20,64,128]{2,1,0:T(8,128)} %get-tuple-element.8) | non-fusion elementwise | flops 163840 | bytes 1966080 | tf_op jit(solution)/shard_map/add | solution.py:597
